TPU v7x, 512 devices: a whole 4x8x8 slice. The times are simulated.
512 devices in a mesh: dp: 16 (over z, core), expert: 8 (over y), sequence: 4 (over x).
Axes of the slice: x: 4, y: 8, z: 8, core: 2. Of those that a mesh axis runs over, the one named last changes fastest.
Arguments:
- tokens: bfloat16 [1536, 3072], P(('dp', 'sequence')), may hold values from -6 to 6
- cotangent: bfloat16 [1536, 3072], P(('dp', 'sequence')), may hold values from -4 to 4
- experts: int32 [1536, 2], P(('dp', 'sequence')), may hold values from 0 to 7, all different within a row; in each aligned block of 24 rows (0 to 23, 24 to 47, ...) at most 10 rows name the same one
- gate_weights: float32 [1536, 2], P(('dp', 'sequence')), may hold values from 0.1 to 1
- w_gate: bfloat16 [8, 8192, 3072], P('expert', ('dp', 'sequence')), may hold values from -0.109375 to 0.109375
- w_up: bfloat16 [8, 8192, 3072], P('expert', ('dp', 'sequence')), may hold values from -0.109375 to 0.109375
- w_down: bfloat16 [8, 8192, 3072], P('expert', ('dp', 'sequence')), may hold values from -0.0625 to 0.0625
Outputs:
- output: bfloat16 [1536, 3072], P(('dp', 'sequence'), 'expert')
- grad_tokens: bfloat16 [1536, 3072], P(('dp', 'sequence'), 'expert')
- grad_w_gate: bfloat16 [8, 8192, 3072], P('expert', ('dp', 'sequence'))
- grad_w_up: bfloat16 [8, 8192, 3072], P('expert', ('dp', 'sequence'))
- grad_w_down: bfloat16 [8, 8192, 3072], P('expert', ('dp', 'sequence'))
Inputs may be any that keep to these rules, and one draw needn't show every extreme that they name: `experts`: A token's two ids differ. Within the rows of one device (aligned blocks of 24 rows) no id is named by more than 10 rows, a bound that some block reaches.
All inputs are finite; a program needn't handle non-finite values.
Results may differ from a plain program's by a relative error of at most 0.019.
Values may be sent and summed in bfloat16 or wider, within the bound.
No kernel may reach another device: no remote copies, remote signals or barrier semaphores. Data moves between devices by JAX's collectives and lax.ppermute only.
A program may use at most 128 MiB of HBM per device.

v0:
```python
import jax
import jax.numpy as jnp
from jax import lax
from jax.sharding import PartitionSpec as P

C = 10
HIGH = lax.Precision.HIGHEST


def on_device(tokens, cotangent, experts, gate_weights, w_gate, w_up, w_down):
    local = w_gate.shape[0]
    model_width = tokens.shape[1]
    first_id = lax.axis_index("expert") * local
    local_ids = first_id + jnp.arange(local, dtype=jnp.int32)
    chosen = (experts[:, :, None] == local_ids[None, None, :]).astype(jnp.int32)
    routed = jnp.sum(chosen, axis=1)
    gate_of = jnp.sum(gate_weights[:, :, None] * chosen.astype(jnp.float32), axis=1)
    slot_of = jnp.cumsum(routed, axis=0) - routed
    slot_ids = jnp.arange(C, dtype=jnp.int32)
    placing = (
        (slot_of.T[:, None, :] == slot_ids[None, :, None]) & (routed.T[:, None, :] == 1)
    ).astype(jnp.float32)
    placing_half = placing.astype(jnp.bfloat16)
    slot_gate = jnp.einsum("ect,te->ec", placing, gate_of, precision=HIGH)
    slot_tokens = jnp.einsum(
        "ect,td->ecd", placing_half, tokens, preferred_element_type=jnp.float32
    ).astype(jnp.bfloat16)
    picked_grad = jnp.einsum(
        "ect,td->ecd", placing_half, cotangent, preferred_element_type=jnp.float32
    )
    scaled_grad = (picked_grad * slot_gate[:, :, None]).astype(jnp.bfloat16)
    dp_count = lax.axis_size("dp")
    seq_count = lax.axis_size("sequence")
    seq_index = lax.axis_index("sequence")
    every_tok, every_grad = (
        lax.all_gather(slot_tokens, ("dp", "sequence"), axis=1, tiled=True),
        lax.all_gather(scaled_grad, ("dp", "sequence"), axis=1, tiled=True),
    )
    grid_tok = every_tok.reshape(local, dp_count, seq_count, C, model_width)
    grid_grad = every_grad.reshape(local, dp_count, seq_count, C, model_width)
    own_tok = lax.dynamic_index_in_dim(grid_tok, seq_index, 2, keepdims=False).reshape(
        local, dp_count * C, model_width
    )
    own_grad = lax.dynamic_index_in_dim(grid_grad, seq_index, 2, keepdims=False).reshape(
        local, dp_count * C, model_width
    )
    gate_rows, up_rows, down_rows = (
        lax.all_gather(w_gate, "sequence", axis=1, tiled=True),
        lax.all_gather(w_up, "sequence", axis=1, tiled=True),
        lax.all_gather(w_down, "sequence", axis=1, tiled=True),
    )
    pre_gate = jnp.einsum("erd,ehd->erh", own_tok, gate_rows, preferred_element_type=jnp.float32)
    pre_up = jnp.einsum("erd,ehd->erh", own_tok, up_rows, preferred_element_type=jnp.float32)
    sigmoid_gate = jax.nn.sigmoid(pre_gate)
    activated = pre_gate * sigmoid_gate
    hidden = (activated * pre_up).astype(jnp.bfloat16)
    out_part = jnp.einsum("erh,ehd->erd", hidden, down_rows, preferred_element_type=jnp.float32)
    out_part = lax.optimization_barrier(out_part.astype(jnp.bfloat16)).astype(jnp.float32)
    grad_hidden = jnp.einsum(
        "erd,ehd->erh", own_grad, down_rows, preferred_element_type=jnp.float32
    )
    grad_gate = (
        grad_hidden * pre_up * sigmoid_gate * (1.0 + pre_gate * (1.0 - sigmoid_gate))
    ).astype(jnp.bfloat16)
    grad_up = (grad_hidden * activated).astype(jnp.bfloat16)
    din_part = jnp.einsum("erh,ehd->erd", grad_gate, gate_rows, preferred_element_type=jnp.float32)
    din_part = din_part + jnp.einsum(
        "erh,ehd->erd", grad_up, up_rows, preferred_element_type=jnp.float32
    )
    din_part = lax.optimization_barrier(din_part.astype(jnp.bfloat16)).astype(jnp.float32)
    gate_cols, up_cols, hidden_cols = (
        lax.all_to_all(grad_gate, "sequence", split_axis=2, concat_axis=1, tiled=True),
        lax.all_to_all(grad_up, "sequence", split_axis=2, concat_axis=1, tiled=True),
        lax.all_to_all(hidden, "sequence", split_axis=2, concat_axis=1, tiled=True),
    )
    block_units = gate_cols.shape[2]
    gate_grid = gate_cols.reshape(local, seq_count, dp_count, C, block_units)
    up_grid = up_cols.reshape(local, seq_count, dp_count, C, block_units)
    hidden_grid = hidden_cols.reshape(local, seq_count, dp_count, C, block_units)
    form = "espch,epscd->ehd"
    grad_w_gate = jnp.einsum(form, gate_grid, grid_tok, preferred_element_type=jnp.float32).astype(
        jnp.bfloat16
    )
    grad_w_up = jnp.einsum(form, up_grid, grid_tok, preferred_element_type=jnp.float32).astype(
        jnp.bfloat16
    )
    grad_w_down = jnp.einsum(
        form, hidden_grid, grid_grad, preferred_element_type=jnp.float32
    ).astype(jnp.bfloat16)
    expert_out, expert_din = (
        lax.psum_scatter(
            out_part.astype(jnp.bfloat16), "dp", scatter_dimension=1, tiled=True
        ).astype(jnp.float32),
        lax.psum_scatter(
            din_part.astype(jnp.bfloat16), "dp", scatter_dimension=1, tiled=True
        ).astype(jnp.float32),
    )
    out_term = jnp.einsum(
        "ect,ecd->td", placing * slot_gate[:, :, None], expert_out, precision=HIGH
    )
    din_term = jnp.einsum("ect,ecd->td", placing, expert_din, precision=HIGH)
    out_total, din_total = (
        lax.psum_scatter(
            out_term.astype(jnp.bfloat16), "expert", scatter_dimension=1, tiled=True
        ).astype(jnp.float32),
        lax.psum_scatter(
            din_term.astype(jnp.bfloat16), "expert", scatter_dimension=1, tiled=True
        ).astype(jnp.float32),
    )
    return (
        out_total.astype(jnp.bfloat16),
        din_total.astype(jnp.bfloat16),
        grad_w_gate,
        grad_w_up,
        grad_w_down,
    )


def solution(mesh):
    return jax.shard_map(
        on_device,
        mesh=mesh,
        in_specs=(
            P(("dp", "sequence"), None),
            P(("dp", "sequence"), None),
            P(("dp", "sequence"), None),
            P(("dp", "sequence"), None),
            P("expert", ("dp", "sequence"), None),
            P("expert", ("dp", "sequence"), None),
            P("expert", ("dp", "sequence"), None),
        ),
        out_specs=(
            P(("dp", "sequence"), "expert"),
            P(("dp", "sequence"), "expert"),
            P("expert", ("dp", "sequence"), None),
            P("expert", ("dp", "sequence"), None),
            P("expert", ("dp", "sequence"), None),
        ),
        check_vma=False,
    )
```

profile of v0, /device:TPU:2, one launch (start us, length us, event | category | flops | bytes accessed | tf_op | source)
XLA Modules:
  0.0 552.4 jit_solution(13933945983895416042)
XLA Ops:
  10.0 1.7 fusion.11
  13.7 88.2 %all-gather.16.cloned.1.call-done = bf16[64,10,3072]{2,1,0:T(8,128)(2,1)} async-done(((bf16[1,10,3072]{2,1,0:T(8,128)(2,1)}), bf16[64,10,3072]{2,1,0:T(8,128)(2,1)}) %all-gather.16.cloned.1.call-update) | async-done | bytes 3932176 | tf_op jit(solution)/shard_map/all_gather | solution.py:36
  103.8 85.1 %all-gather.18.cloned.1.call-done = bf16[64,10,3072]{2,1,0:T(8,128)(2,1)} async-done(((bf16[1,10,3072]{2,1,0:T(8,128)(2,1)}), bf16[64,10,3072]{2,1,0:T(8,128)(2,1)}) %all-gather.18.cloned.1.call-update) | async-done | bytes 3932176 | tf_op jit(solution)/shard_map/all_gather | solution.py:37
  191.7 41.3 %all-gather.10.cloned.1.call-done = bf16[1,512,3072]{2,1,0:T(8,128)(2,1)} async-done(((bf16[1,128,3072]{2,1,0:T(8,128)(2,1)}), bf16[1,512,3072]{2,1,0:T(8,128)(2,1)}) %all-gather.10.cloned.1.call-update) | async-done | bytes 3145744 | tf_op jit(solution)/shard_map/all_gather | solution.py:48
  232.9 3.1 fusion.20
  236.0 43.9 %all-gather.12.cloned.1.call-done = bf16[1,512,3072]{2,1,0:T(8,128)(2,1)} async-done(((bf16[1,128,3072]{2,1,0:T(8,128)(2,1)}), bf16[1,512,3072]{2,1,0:T(8,128)(2,1)}) %all-gather.12.cloned.1.call-update) | async-done | bytes 3145744 | tf_op jit(solution)/shard_map/all_gather | solution.py:49
  280.0 3.1 fusion.16
  283.0 43.9 %all-gather.14.cloned.1.call-done = bf16[1,512,3072]{2,1,0:T(8,128)(2,1)} async-done(((bf16[1,128,3072]{2,1,0:T(8,128)(2,1)}), bf16[1,512,3072]{2,1,0:T(8,128)(2,1)}) %all-gather.14.cloned.1.call-update) | async-done | bytes 3145744 | tf_op jit(solution)/shard_map/all_gather | solution.py:50
  327.0 3.3 multiply_convert_fusion
  330.3 1.7 fusion.5
  334.0 1.7 fusion.4
  336.7 2.3 reduce.5
  340.1 4.6 all-to-all-start
  347.1 2.3 reduce.6
  350.5 4.8 all-to-all-start.1
  355.8 2.3 reduce.7
  360.1 4.8 all-to-all-start.2
  365.7 4.7 fusion.8
  370.4 88.1 %all-reduce.5.cloned.1.call-done = (bf16[1,160,3072]{2,1,0:T(8,128)(2,1)}, bf16[1,160,3072]{2,1,0:T(8,128)(2,1)}) async-done(((bf16[1,160,3072]{2,1,0:T(8,128)(2,1)}, bf16[1,160,3072]{2,1,0:T(8,128)(2,1)}), (bf16[1,160,3072]{2,1,0:T(8,128)(2,1)}, bf16[1,160,3072]{2,1,0:T(8,128)(2,1)})) %all-reduce.5.cloned.1.call-update) | async-done | bytes 1966096
  461.0 4.7 fusion.7
  468.9 4.7 fusion.6
  473.6 27.9 %reduce-scatter.9.cloned.1.call-done = bf16[384,24]{1,0:T(8,128)(2,1)} async-done(((bf16[3072,24]{1,0:T(8,128)(2,1)}), bf16[384,24]{1,0:T(8,128)(2,1)}) %reduce-scatter.9.cloned.1.call-update) | async-done | bytes 18448
  503.0 41.0 %reduce-scatter.11.cloned.1.call-done = bf16[384,24]{1,0:T(8,128)(2,1)} async-done(((bf16[3072,24]{1,0:T(8,128)(2,1)}), bf16[384,24]{1,0:T(8,128)(2,1)}) %reduce-scatter.11.cloned.1.call-update) | async-done | bytes 18448
  544.0 1.6 copy.59
  (66 shorter events, 26.6 us)
Async XLA Ops:
  7.2 1.1 copy-start
  7.2 94.7 %all-gather.16.cloned.1.call-start = ((), (), s32[]{:S(2)}) async-start(), calls=%async_computation.8 | async-start | bytes 6389760 | tf_op jit(solution)/shard_map/all_gather | solution.py:36
  9.1 179.9 %all-gather.18.cloned.1.call-start = ((), (), s32[]{:S(2)}) async-start(), calls=%async_computation.9 | async-start | bytes 6389760 | tf_op jit(solution)/shard_map/all_gather | solution.py:37
  11.7 221.2 %all-gather.10.cloned.1.call-start = ((), (), s32[]{:S(2)}) async-start(), calls=%async_computation.5 | async-start | bytes 3932160 | tf_op jit(solution)/shard_map/all_gather | solution.py:48
  12.4 267.5 %all-gather.12.cloned.1.call-start = ((), (), s32[]{:S(2)}) async-start(), calls=%async_computation.6 | async-start | bytes 3932160 | tf_op jit(solution)/shard_map/all_gather | solution.py:49
  13.0 314.0 %all-gather.14.cloned.1.call-start = ((), (), s32[]{:S(2)}) async-start(), calls=%async_computation.7 | async-start | bytes 3932160 | tf_op jit(solution)/shard_map/all_gather | solution.py:50
  13.6 444.9 %all-reduce.5.cloned.1.call-start = ((), (), s32[]{:S(2)}) async-start(), calls=%async_computation.12 | async-start | bytes 3932160
  236.0 91.0 %copy-start.4 = (bf16[160,3072]{1,0:T(8,128)(2,1)S(1)}, bf16[160,3072]{1,0:T(8,128)(2,1)}, u32[]{:S(2)}) copy-start(bf16[160,3072]{1,0:T(8,128)(2,1)} %reshape.384) | copy-start | bytes 2949124
  327.0 3.3 copy-start.3
  330.3 2.2 copy-start.1
  332.0 2.0 copy-start.2
  340.1 10.4 %all-to-all-start = ((bf16[4,2,10240]{2,1,0:T(2,128)(2,1)}), bf16[4,2,10240]{2,1,0:T(2,128)(2,1)S(1)}, u32[]{:S(2)}, u32[]{:S(2)}) async-start(bf16[4,2,10240]{2,1,0:T(2,128)(2,1)} %reshape.421), calls=%async_computation | async-start | bytes 327680 | tf_op jit(solution)/shard_map/all_to_all | solution.py:72
  350.5 9.6 %all-to-all-start.1 = ((bf16[4,2,10240]{2,1,0:T(2,128)(2,1)}), bf16[4,2,10240]{2,1,0:T(2,128)(2,1)S(1)}, u32[]{:S(2)}, u32[]{:S(2)}) async-start(bf16[4,2,10240]{2,1,0:T(2,128)(2,1)} %reshape.423), calls=%async_computation.1 | async-start | bytes 327680 | tf_op jit(solution)/shard_map/all_to_all | solution.py:73
  360.1 105.6 %all-to-all-start.2 = ((bf16[4,2,10240]{2,1,0:T(2,128)(2,1)}), bf16[4,2,10240]{2,1,0:T(2,128)(2,1)S(1)}, u32[]{:S(2)}, u32[]{:S(2)}) async-start(bf16[4,2,10240]{2,1,0:T(2,128)(2,1)} %reshape.425), calls=%async_computation.2 | async-start | bytes 327680 | tf_op jit(solution)/shard_map/all_to_all | solution.py:74
  364.9 136.6 %reduce-scatter.9.cloned.1.call-start = ((), (), s32[]{:S(2)}) async-start(), calls=%async_computation.10 | async-start | bytes 884736
  461.0 83.1 %reduce-scatter.11.cloned.1.call-start = ((), (), s32[]{:S(2)}) async-start(), calls=%async_computation.11 | async-start | bytes 884736
Sparse Core Ops, SparseCore 0:
  11.9 89.9 all-gather.15
  105.8 83.1 all-gather.17
  191.0 41.8 all-gather.9
  234.9 45.0 all-gather.11
  281.9 45.0 all-gather.13
  335.8 122.6 all-reduce.4
  461.3 40.0 reduce-scatter.8
  504.3 39.6 reduce-scatter.10
where the time goes:
time: 553 us; the launch traced here: 552 us
  waiting for transfers between devices  461 us (83%)
  matrix products  32.6 us (6%)
  local copies, waits for them, and re-layouts  20.4 us (4%)
  between operations  15 us (3%)
  starting transfers between devices  14.5 us (3%)
  other arithmetic  8.64 us (2%)
    unnamed x11, waiting for transfers between devices  159 us
    all_gather x1, waiting for transfers between devices, on_device(): lax.all_gather(slot_tokens, ('dp', 'sequence'), axis=1, tiled=True)  88.2 us
    all_gather x1, waiting for transfers between devices, on_device(): lax.all_gather(scaled_grad, ('dp', 'sequence'), axis=1, tiled=True)  85.1 us
    all_gather x1, waiting for transfers between devices, on_device(): lax.all_gather(w_down, 'sequence', axis=1, tiled=True)  43.9 us
    all_gather x1, waiting for transfers between devices, on_device(): lax.all_gather(w_up, 'sequence', axis=1, tiled=True)  43.9 us
    all_gather x1, waiting for transfers between devices, on_device(): lax.all_gather(w_gate, 'sequence', axis=1, tiled=True)  41.3 us
    unnamed x24, local copies, waits for them, and re-layouts  16.3 us
  transfers between devices with their start and end apart: 11, of which 8 were waited for; matrix products, arithmetic and copies ran while one was open for 9% of the time, Pallas kernels for 0%

commit v1 on v0

--- a/solution.py
+++ b/solution.py
@@ -5,6 +5,11 @@
 
 C = 10
 HIGH = lax.Precision.HIGHEST
+
+
+def swapped_in(block, name, dim):
+    sent = jnp.stack([block] * lax.axis_size(name))
+    return jnp.concatenate(lax.all_to_all(sent, name, 0, 0), axis=dim)
 
 
 def on_device(tokens, cotangent, experts, gate_weights, w_gate, w_up, w_down):
@@ -46,7 +51,7 @@
     )
     gate_rows, up_rows, down_rows = (
         lax.all_gather(w_gate, "sequence", axis=1, tiled=True),
-        lax.all_gather(w_up, "sequence", axis=1, tiled=True),
+        swapped_in(w_up, "sequence", 1),
         lax.all_gather(w_down, "sequence", axis=1, tiled=True),
     )
     pre_gate = jnp.einsum("erd,ehd->erh", own_tok, gate_rows, preferred_element_type=jnp.float32)

time: 553 us -> 518 us (0.937)
  waiting for transfers between devices: 461 us -> 405 us
  starting transfers between devices: 14.5 us -> 24 us
  local copies, waits for them, and re-layouts: 20.4 us -> 29.4 us
    all_gather x1 -> x0, waiting for transfers between devices: 43.9 us -> none  [on_device(): lax.all_gather(w_up, 'sequence', axis=1, tiled=True)]
    all_to_all x0 -> x1, starting transfers between devices: none -> 9.55 us  [swapped_in(): return jnp.concatenate(lax.all_to_all(sent, name, 0, 0), axis=dim)]
    another operation x3 -> x4, local copies, waits for them, and re-layouts: 1.66 us -> 7.95 us
    all_gather x1, waiting for transfers between devices: 41.3 us -> 35.7 us  [on_device(): lax.all_gather(w_gate, 'sequence', axis=1, tiled=True)]
    unnamed x24 -> x26, local copies, waits for them, and re-layouts: 16.3 us -> 18.2 us
    unnamed x11 -> x10, waiting for transfers between devices: 159 us -> 157 us
  transfers between devices with their start and end apart: 11 -> 11, of which waited for: 8 -> 7; matrix products, arithmetic and copies ran while one was open for 9% -> 12% of each run, Pallas kernels for 0% -> 0%
where the time goes in v1:
time: 518 us; the launch traced here: 516 us
  waiting for transfers between devices  405 us (78%)
  matrix products  34.1 us (7%)
  local copies, waits for them, and re-layouts  29.4 us (6%)
  starting transfers between devices  24 us (5%)
  between operations  15 us (3%)
  other arithmetic  8.64 us (2%)
    unnamed x10, waiting for transfers between devices  157 us
    all_gather x1, waiting for transfers between devices, on_device(): lax.all_gather(slot_tokens, ('dp', 'sequence'), axis=1, tiled=True)  87.5 us
    all_gather x1, waiting for transfers between devices, on_device(): lax.all_gather(scaled_grad, ('dp', 'sequence'), axis=1, tiled=True)  82 us
    all_gather x1, waiting for transfers between devices, on_device(): lax.all_gather(w_down, 'sequence', axis=1, tiled=True)  42.9 us
    all_gather x1, waiting for transfers between devices, on_device(): lax.all_gather(w_gate, 'sequence', axis=1, tiled=True)  35.7 us
    unnamed x26, local copies, waits for them, and re-layouts  18.2 us
  transfers between devices with their start and end apart: 11, of which 7 were waited for; matrix products, arithmetic and copies ran while one was open for 12% of the time, Pallas kernels for 0%

profile of v1, /device:TPU:2, one launch (start us, length us, event | category | flops | bytes accessed | tf_op | source)
XLA Modules:
  0.0 516.4 jit_solution(13842493015867050518)
XLA Ops:
  13.0 3.2 stack.2
  16.2 9.5 %all-to-all-start = ((bf16[4,1,128,3072]{3,2,1,0:T(8,128)(2,1)}), bf16[4,1,128,3072]{3,2,1,0:T(8,128)(2,1)S(1)}, u32[]{:S(2)}, u32[]{:S(2)}) async-start(bf16[4,1,128,3072]{3,2,1,0:T(8,128)(2,1)} %stack.2), calls=%async_computation | async-start | bytes 6291456 | tf_op jit(solution)/shard_map/all_to_all | solution.py:12
  25.7 87.5 %all-gather.13.cloned.1.call-done = bf16[64,10,3072]{2,1,0:T(8,128)(2,1)} async-done(((bf16[1,10,3072]{2,1,0:T(8,128)(2,1)}), bf16[64,10,3072]{2,1,0:T(8,128)(2,1)}) %all-gather.13.cloned.1.call-update) | async-done | bytes 3932176 | tf_op jit(solution)/shard_map/all_gather | solution.py:41
  113.2 2.8 dynamic-slice_bitcast_fusion.1
  118.3 82.0 %all-gather.15.cloned.1.call-done = bf16[64,10,3072]{2,1,0:T(8,128)(2,1)} async-done(((bf16[1,10,3072]{2,1,0:T(8,128)(2,1)}), bf16[64,10,3072]{2,1,0:T(8,128)(2,1)}) %all-gather.15.cloned.1.call-update) | async-done | bytes 3932176 | tf_op jit(solution)/shard_map/all_gather | solution.py:42
  200.3 2.8 dynamic-slice_bitcast_fusion
  203.0 2.4 reshape.390
  205.4 3.1 fusion.40
  208.6 35.7 %all-gather.9.cloned.1.call-done = bf16[1,512,3072]{2,1,0:T(8,128)(2,1)} async-done(((bf16[1,128,3072]{2,1,0:T(8,128)(2,1)}), bf16[1,512,3072]{2,1,0:T(8,128)(2,1)}) %all-gather.9.cloned.1.call-update) | async-done | bytes 3145744 | tf_op jit(solution)/shard_map/all_gather | solution.py:53
  244.3 4.1 fusion.17
  248.4 42.9 %all-gather.11.cloned.1.call-done = bf16[1,512,3072]{2,1,0:T(8,128)(2,1)} async-done(((bf16[1,128,3072]{2,1,0:T(8,128)(2,1)}), bf16[1,512,3072]{2,1,0:T(8,128)(2,1)}) %all-gather.11.cloned.1.call-update) | async-done | bytes 3145744 | tf_op jit(solution)/shard_map/all_gather | solution.py:55
  291.3 3.7 multiply_convert_fusion
  301.7 2.3 reduce.5
  305.1 4.6 all-to-all-start.1
  312.1 2.3 reduce.6
  315.6 4.8 all-to-all-start.2
  320.9 2.3 reduce.7
  325.1 4.8 all-to-all-start.3
  330.8 4.7 fusion.8
  335.5 87.1 %all-reduce.5.cloned.1.call-done = (bf16[1,160,3072]{2,1,0:T(8,128)(2,1)}, bf16[1,160,3072]{2,1,0:T(8,128)(2,1)}) async-done(((bf16[1,160,3072]{2,1,0:T(8,128)(2,1)}, bf16[1,160,3072]{2,1,0:T(8,128)(2,1)}), (bf16[1,160,3072]{2,1,0:T(8,128)(2,1)}, bf16[1,160,3072]{2,1,0:T(8,128)(2,1)})) %all-reduce.5.cloned.1.call-update) | async-done | bytes 1966096
  425.2 4.7 fusion.7
  433.1 4.7 fusion.6
  437.7 27.7 %reduce-scatter.9.cloned.1.call-done = bf16[384,24]{1,0:T(8,128)(2,1)} async-done(((bf16[3072,24]{1,0:T(8,128)(2,1)}), bf16[384,24]{1,0:T(8,128)(2,1)}) %reduce-scatter.9.cloned.1.call-update) | async-done | bytes 18448
  467.1 41.0 %reduce-scatter.11.cloned.1.call-done = bf16[384,24]{1,0:T(8,128)(2,1)} async-done(((bf16[3072,24]{1,0:T(8,128)(2,1)}), bf16[384,24]{1,0:T(8,128)(2,1)}) %reduce-scatter.11.cloned.1.call-update) | async-done | bytes 18448
  (68 shorter events, 30.6 us)
Async XLA Ops:
  7.2 1.1 copy-start
  7.2 106.0 %all-gather.13.cloned.1.call-start = ((), (), s32[]{:S(2)}) async-start(), calls=%async_computation.8 | async-start | bytes 6389760 | tf_op jit(solution)/shard_map/all_gather | solution.py:41
  9.1 191.2 %all-gather.15.cloned.1.call-start = ((), (), s32[]{:S(2)}) async-start(), calls=%async_computation.9 | async-start | bytes 6389760 | tf_op jit(solution)/shard_map/all_gather | solution.py:42
  11.7 232.6 %all-gather.9.cloned.1.call-start = ((), (), s32[]{:S(2)}) async-start(), calls=%async_computation.6 | async-start | bytes 3932160 | tf_op jit(solution)/shard_map/all_gather | solution.py:53
  12.4 278.9 %all-gather.11.cloned.1.call-start = ((), (), s32[]{:S(2)}) async-start(), calls=%async_computation.7 | async-start | bytes 3932160 | tf_op jit(solution)/shard_map/all_gather | solution.py:55
  16.2 189.2 %all-to-all-start = ((bf16[4,1,128,3072]{3,2,1,0:T(8,128)(2,1)}), bf16[4,1,128,3072]{3,2,1,0:T(8,128)(2,1)S(1)}, u32[]{:S(2)}, u32[]{:S(2)}) async-start(bf16[4,1,128,3072]{3,2,1,0:T(8,128)(2,1)} %stack.2), calls=%async_computation | async-start | bytes 6291456 | tf_op jit(solution)/shard_map/all_to_all | solution.py:12
  25.7 396.9 %all-reduce.5.cloned.1.call-start = ((), (), s32[]{:S(2)}) async-start(), calls=%async_computation.12 | async-start | bytes 3932160
  291.3 3.8 copy-start.2
  295.0 3.1 copy-start.5
  295.1 3.1 copy-start.3
  295.1 2.4 copy-start.1
  299.9 11.8 %copy-start.4 = (bf16[160,512]{1,0:T(8,128)(2,1)S(1)}, bf16[160,512]{1,0:T(8,128)(2,1)}, u32[]{:S(2)}) copy-start(bf16[160,512]{1,0:T(8,128)(2,1)} %copy-done.3) | copy-start | bytes 491524
  305.1 10.4 %all-to-all-start.1 = ((bf16[4,2,10240]{2,1,0:T(2,128)(2,1)}), bf16[4,2,10240]{2,1,0:T(2,128)(2,1)S(1)}, u32[]{:S(2)}, u32[]{:S(2)}) async-start(bf16[4,2,10240]{2,1,0:T(2,128)(2,1)} %reshape.427), calls=%async_computation.1 | async-start | bytes 327680 | tf_op jit(solution)/shard_map/all_to_all | solution.py:77
  315.6 9.6 %all-to-all-start.2 = ((bf16[4,2,10240]{2,1,0:T(2,128)(2,1)}), bf16[4,2,10240]{2,1,0:T(2,128)(2,1)S(1)}, u32[]{:S(2)}, u32[]{:S(2)}) async-start(bf16[4,2,10240]{2,1,0:T(2,128)(2,1)} %reshape.429), calls=%async_computation.2 | async-start | bytes 327680 | tf_op jit(solution)/shard_map/all_to_all | solution.py:78
  325.1 104.7 %all-to-all-start.3 = ((bf16[4,2,10240]{2,1,0:T(2,128)(2,1)}), bf16[4,2,10240]{2,1,0:T(2,128)(2,1)S(1)}, u32[]{:S(2)}, u32[]{:S(2)}) async-start(bf16[4,2,10240]{2,1,0:T(2,128)(2,1)} %reshape.431), calls=%async_computation.3 | async-start | bytes 327680 | tf_op jit(solution)/shard_map/all_to_all | solution.py:79
  330.0 135.5 %reduce-scatter.9.cloned.1.call-start = ((), (), s32[]{:S(2)}) async-start(), calls=%async_computation.10 | async-start | bytes 884736
  425.1 82.9 %reduce-scatter.11.cloned.1.call-start = ((), (), s32[]{:S(2)}) async-start(), calls=%async_computation.11 | async-start | bytes 884736
Sparse Core Ops, SparseCore 0:
  11.9 101.2 all-gather.12
  117.1 83.1 all-gather.14
  202.4 41.8 all-gather.8
  246.2 45.0 all-gather.10
  300.0 122.6 all-reduce.4
  425.3 40.0 reduce-scatter.8
  468.3 39.6 reduce-scatter.10
